TPU v7x, 32 devices: a whole 2x2x4 slice. The times are simulated.
32 devices in a mesh: dp: 8 (over y, x, core), tensor: 4 (over z).
Axes of the slice: x: 2, y: 2, z: 4, core: 2. Of those that a mesh axis runs over, the one named last changes fastest.
Arguments:
- tokens_in: bfloat16 [8192, 1536], P('dp'), may hold values from -6 to 6
- doc_ids: int32 [8192], replicated, may hold values from 0 to 3, never falling along the last dimension, each value on 1 to 4096 neighbouring positions
- out_grad: bfloat16 [8192, 1536], P('dp'), may hold values from -6 to 6
- norm_gains: bfloat16 [2, 1536], replicated, may hold values from 0.5 to 1.5
- conv_taps: bfloat16 [3, 1536], P(None, 'tensor'), may hold values from -3.5 to 3.5
- stream_weight: bfloat16 [3, 1536, 1536], P(None, None, 'tensor'), may hold values from -0.15625 to 0.15625
- mixer_weight: bfloat16 [1536, 1536], P('tensor'), may hold values from -0.15625 to 0.15625
- hidden_weight: bfloat16 [2, 1536, 6912], P(None, None, 'tensor'), may hold values from -0.15625 to 0.15625
- down_weight: bfloat16 [6912, 1536], P('tensor'), may hold values from -0.078125 to 0.078125
- gains_first: float32 [2, 1536], replicated, may hold values from -0.0009336855 to 0.0009336855
- gains_second: float32 [2, 1536], replicated, may hold values from 7.2647386e-09 to 7.264739e-08
- taps_first: float32 [3, 1536], P(None, 'tensor'), may hold values from -0.0009336855 to 0.0009336855
- taps_second: float32 [3, 1536], P(None, 'tensor'), may hold values from 7.2647386e-09 to 7.264739e-08
- stream_first: float32 [3, 1536, 1536], P(None, 'dp', 'tensor'), may hold values from -0.0009336855 to 0.0009336855
- stream_second: float32 [3, 1536, 1536], P(None, 'dp', 'tensor'), may hold values from 7.2647386e-09 to 7.264739e-08
- mixer_first: float32 [1536, 1536], P('tensor', 'dp'), may hold values from -0.0009336855 to 0.0009336855
- mixer_second: float32 [1536, 1536], P('tensor', 'dp'), may hold values from 7.2647386e-09 to 7.264739e-08
- hidden_first: float32 [2, 1536, 6912], P(None, 'dp', 'tensor'), may hold values from -0.0009336855 to 0.0009336855
- hidden_second: float32 [2, 1536, 6912], P(None, 'dp', 'tensor'), may hold values from 7.2647386e-09 to 7.264739e-08
- down_first: float32 [6912, 1536], P('tensor', 'dp'), may hold values from -0.0009336855 to 0.0009336855
- down_second: float32 [6912, 1536], P('tensor', 'dp'), may hold values from 7.2647386e-09 to 7.264739e-08
Outputs:
- block_out: bfloat16 [8192, 1536], P('dp')
- input_grad: float32 [8192, 1536], P('dp')
- grad_norm: float32 [], replicated
- gains_grad: float32 [2, 1536], replicated
- gains_first_next: float32 [2, 1536], replicated
- gains_second_next: float32 [2, 1536], replicated
- gains_step: float32 [2, 1536], replicated
- taps_grad: float32 [3, 1536], P(None, 'tensor')
- taps_first_next: float32 [3, 1536], P(None, 'tensor')
- taps_second_next: float32 [3, 1536], P(None, 'tensor')
- taps_step: float32 [3, 1536], P(None, 'tensor')
- stream_grad: float32 [3, 1536, 1536], P(None, 'dp', 'tensor')
- stream_first_next: float32 [3, 1536, 1536], P(None, 'dp', 'tensor')
- stream_second_next: float32 [3, 1536, 1536], P(None, 'dp', 'tensor')
- stream_step: float32 [3, 1536, 1536], P(None, 'dp', 'tensor')
- mixer_grad: float32 [1536, 1536], P('tensor', 'dp')
- mixer_first_next: float32 [1536, 1536], P('tensor', 'dp')
- mixer_second_next: float32 [1536, 1536], P('tensor', 'dp')
- mixer_step: float32 [1536, 1536], P('tensor', 'dp')
- hidden_grad: float32 [2, 1536, 6912], P(None, 'dp', 'tensor')
- hidden_first_next: float32 [2, 1536, 6912], P(None, 'dp', 'tensor')
- hidden_second_next: float32 [2, 1536, 6912], P(None, 'dp', 'tensor')
- hidden_step: float32 [2, 1536, 6912], P(None, 'dp', 'tensor')
- down_grad: float32 [6912, 1536], P('tensor', 'dp')
- down_first_next: float32 [6912, 1536], P('tensor', 'dp')
- down_second_next: float32 [6912, 1536], P('tensor', 'dp')
- down_step: float32 [6912, 1536], P('tensor', 'dp')
Inputs may be any that keep to these rules, and one draw needn't show every extreme that they name: `doc_ids`: document ids never fall along the tokens; each document has 1 to 4096 tokens, and one has exactly 4096.
All inputs are finite; a program needn't handle non-finite values.
Results may differ from a plain program's by a relative error of at most 0.01.
The roundings to bfloat16 on the way count: a program that leaves them out, or rounds other values in their place, can miss the bound.
Values may be sent and summed in bfloat16 or wider, within the bound.
A program may use at most 256 MiB of HBM per device.

v0:
```python
import jax
import jax.numpy as jnp
from jax import lax
from jax.sharding import PartitionSpec as P

EPS_NORM = 1e-05
LEARN_RATE = 0.02
BETA_FIRST = 0.5
BETA_SECOND = 0.5
CORRECTION = 1.0 - 0.5**3
ADAM_EPS = 1e-08
DECAY_RATE = 0.1
CLIP_NORM = 1.0


def shifted(value, axis, steps):
    count = lax.axis_size(axis)
    leading, last = (max(0, -steps), min(count, count - steps))
    return lax.ppermute(value, axis, [(source, source + steps) for source in range(leading, last)])


def rms_scale(values):
    return lax.rsqrt(jnp.mean(values * values, axis=-1, keepdims=True) + EPS_NORM)


def norm_back(grad_normed, normal, inverse, gain_row):
    scaled = grad_normed * gain_row
    return inverse * (scaled - normal * jnp.mean(scaled * normal, axis=-1, keepdims=True))


def adam_step(master, gradient, first_moment, second_moment, factor, decay):
    clipped = gradient * factor
    first_next = BETA_FIRST * first_moment + (1.0 - BETA_FIRST) * clipped
    second_next = BETA_SECOND * second_moment + (1.0 - BETA_SECOND) * clipped * clipped
    change = -LEARN_RATE * (
        first_next / CORRECTION / (jnp.sqrt(second_next / CORRECTION) + ADAM_EPS) + decay * master
    )
    return (first_next, second_next, change)


def own_share(weight, share):
    offset_row = lax.axis_index("dp") * share
    return lax.dynamic_slice_in_dim(weight, offset_row, share, 1).astype(jnp.float32)


def contract_rows(left, right):
    return lax.dot_general(
        left, right, (((0,), (0,)), ((), ())), preferred_element_type=jnp.float32
    )


def contract_cols(left, right):
    return lax.dot_general(
        left, right, (((1,), (1,)), ((), ())), preferred_element_type=jnp.float32
    )


def squares(values):
    return jnp.sum(values * values)


def body(
    tokens_in,
    doc_ids,
    out_grad,
    norm_gains,
    conv_taps,
    stream_weight,
    mixer_weight,
    hidden_weight,
    down_weight,
    gains_first,
    gains_second,
    taps_first,
    taps_second,
    stream_first,
    stream_second,
    mixer_first,
    mixer_second,
    hidden_first,
    hidden_second,
    down_first,
    down_second,
):
    tok_rows = tokens_in.shape[0]
    kernel = conv_taps.shape[0]
    reach = kernel - 1
    first_row = lax.axis_index("dp") * tok_rows
    filler = jnp.full((reach,), -1, jnp.int32)
    padded_ids = jnp.concatenate([filler, doc_ids, filler])
    window = lax.dynamic_slice_in_dim(padded_ids, first_row, tok_rows + 2 * reach)
    current = window[reach : reach + tok_rows]
    back_valid = [
        (window[reach - offset : reach - offset + tok_rows] == current).astype(jnp.float32)[:, None]
        for offset in range(kernel)
    ]
    ahead_valid = [
        (window[reach + offset : reach + offset + tok_rows] == current).astype(jnp.float32)[:, None]
        for offset in range(kernel)
    ]
    tokens = tokens_in.astype(jnp.float32)
    gain_pair = norm_gains.astype(jnp.float32)
    tap_values = conv_taps.astype(jnp.float32)
    scale_one = rms_scale(tokens)
    normal_one = tokens * scale_one
    normed_one = (normal_one * gain_pair[0]).astype(jnp.bfloat16)
    streams = jnp.einsum(
        "td,sdc->stc", normed_one, stream_weight, preferred_element_type=jnp.float32
    )
    product = (streams[0] * streams[2]).astype(jnp.bfloat16)
    edge_rows = shifted(product[tok_rows - reach :], "dp", 1)
    extended = jnp.concatenate([edge_rows, product], 0).astype(jnp.float32)
    conv_out = tap_values[0] * extended[reach : reach + tok_rows] * back_valid[0]
    for offset in range(1, kernel):
        conv_out = (
            conv_out
            + tap_values[offset]
            * extended[reach - offset : reach - offset + tok_rows]
            * back_valid[offset]
        )
    gated_rows = (streams[1] * conv_out).astype(jnp.bfloat16)
    branch_part = jnp.dot(gated_rows, mixer_weight, preferred_element_type=jnp.float32)
    branch = lax.psum(branch_part, "tensor")
    middle = tokens + branch
    scale_two = rms_scale(middle)
    normal_two = middle * scale_two
    normed_two = (normal_two * gain_pair[1]).astype(jnp.bfloat16)
    hidden = jnp.einsum(
        "td,sdf->stf", normed_two, hidden_weight, preferred_element_type=jnp.float32
    )
    sigmoid_gate = jax.nn.sigmoid(hidden[0])
    silu_gate = hidden[0] * sigmoid_gate
    active = (silu_gate * hidden[1]).astype(jnp.bfloat16)
    feed_part = jnp.dot(active, down_weight, preferred_element_type=jnp.float32)
    feed_out = lax.psum(feed_part.astype(jnp.bfloat16), "tensor").astype(jnp.float32)
    block_out = (middle + feed_out).astype(jnp.bfloat16)
    upstream = out_grad.astype(jnp.float32)
    down_part = contract_rows(active, out_grad)
    grad_active = contract_cols(out_grad, down_weight)
    grad_gate = grad_active * hidden[1] * sigmoid_gate * (1.0 + hidden[0] * (1.0 - sigmoid_gate))
    grad_up = grad_active * silu_gate
    grad_hidden = jnp.stack([grad_gate, grad_up]).astype(jnp.bfloat16)
    hidden_part = jnp.einsum(
        "td,stf->sdf", normed_two, grad_hidden, preferred_element_type=jnp.float32
    )
    normed_two_part = jnp.einsum(
        "stf,sdf->td", grad_hidden, hidden_weight, preferred_element_type=jnp.float32
    )
    grad_normed_two = lax.psum(normed_two_part, "tensor")
    gain_two_part = jnp.sum(grad_normed_two * normal_two, axis=0)
    grad_middle = upstream + norm_back(grad_normed_two, normal_two, scale_two, gain_pair[1])
    grad_branch = grad_middle.astype(jnp.bfloat16)
    mixer_part = contract_rows(gated_rows, grad_branch)
    grad_gated = contract_cols(grad_branch, mixer_weight)
    grad_c = grad_gated * conv_out
    grad_conv = (grad_gated * streams[1]).astype(jnp.bfloat16)
    ahead_rows = shifted(grad_conv[:reach], "dp", -1)
    trailing = jnp.concatenate([grad_conv, ahead_rows], 0).astype(jnp.float32)
    grad_conv_wide = trailing[:tok_rows]
    taps_part = jnp.stack(
        [
            jnp.sum(
                grad_conv_wide
                * extended[reach - offset : reach - offset + tok_rows]
                * back_valid[offset],
                axis=0,
            )
            for offset in range(kernel)
        ]
    )
    grad_product = tap_values[0] * grad_conv_wide * ahead_valid[0]
    for offset in range(1, kernel):
        grad_product = (
            grad_product
            + tap_values[offset] * trailing[offset : offset + tok_rows] * ahead_valid[offset]
        )
    grad_streams = jnp.stack([grad_product * streams[2], grad_c, grad_product * streams[0]]).astype(
        jnp.bfloat16
    )
    stream_part = jnp.einsum(
        "td,stc->sdc", normed_one, grad_streams, preferred_element_type=jnp.float32
    )
    normed_one_part = jnp.einsum(
        "stc,sdc->td", grad_streams, stream_weight, preferred_element_type=jnp.float32
    )
    grad_normed_one = lax.psum(normed_one_part, "tensor")
    gain_one_part = jnp.sum(grad_normed_one * normal_one, axis=0)
    input_grad = grad_middle + norm_back(grad_normed_one, normal_one, scale_one, gain_pair[0])
    gain_stack = jnp.stack([gain_one_part, gain_two_part])
    gains_grad, taps_grad = lax.psum((gain_stack, taps_part), "dp")
    stream_total, mixer_total, hidden_total, down_total = (
        lax.psum_scatter(stream_part, "dp", scatter_dimension=1, tiled=True),
        lax.psum_scatter(mixer_part, "dp", scatter_dimension=1, tiled=True),
        lax.psum_scatter(hidden_part, "dp", scatter_dimension=1, tiled=True),
        lax.psum_scatter(down_part, "dp", scatter_dimension=1, tiled=True),
    )
    first_dp = (lax.axis_index("dp") == 0).astype(jnp.float32)
    first_tensor = (lax.axis_index("tensor") == 0).astype(jnp.float32)
    local_square = (
        squares(stream_total) + squares(mixer_total) + squares(hidden_total) + squares(down_total)
    )
    local_square = local_square + first_dp * (
        squares(taps_grad) + first_tensor * squares(gains_grad)
    )
    square_total = lax.psum(local_square, ("dp", "tensor"))
    grad_norm = jnp.sqrt(square_total)
    factor = jnp.minimum(1.0, CLIP_NORM / (grad_norm + 1e-06))
    gains_out = adam_step(gain_pair, gains_grad, gains_first, gains_second, factor, 0.0)
    taps_out = adam_step(tap_values, taps_grad, taps_first, taps_second, factor, DECAY_RATE)
    stream_out = adam_step(
        own_share(stream_weight, stream_total.shape[1]),
        stream_total,
        stream_first,
        stream_second,
        factor,
        DECAY_RATE,
    )
    mixer_out = adam_step(
        own_share(mixer_weight, mixer_total.shape[1]),
        mixer_total,
        mixer_first,
        mixer_second,
        factor,
        DECAY_RATE,
    )
    hidden_out = adam_step(
        own_share(hidden_weight, hidden_total.shape[1]),
        hidden_total,
        hidden_first,
        hidden_second,
        factor,
        DECAY_RATE,
    )
    down_out = adam_step(
        own_share(down_weight, down_total.shape[1]),
        down_total,
        down_first,
        down_second,
        factor,
        DECAY_RATE,
    )
    return (
        block_out,
        input_grad,
        grad_norm,
        gains_grad,
        gains_out[0],
        gains_out[1],
        gains_out[2],
        taps_grad,
        taps_out[0],
        taps_out[1],
        taps_out[2],
        stream_total,
        stream_out[0],
        stream_out[1],
        stream_out[2],
        mixer_total,
        mixer_out[0],
        mixer_out[1],
        mixer_out[2],
        hidden_total,
        hidden_out[0],
        hidden_out[1],
        hidden_out[2],
        down_total,
        down_out[0],
        down_out[1],
        down_out[2],
    )


def solution(mesh):
    return jax.shard_map(
        body,
        mesh=mesh,
        in_specs=(
            P("dp", None),
            P(),
            P("dp", None),
            P(),
            P(None, "tensor"),
            P(None, None, "tensor"),
            P("tensor", None),
            P(None, None, "tensor"),
            P("tensor", None),
            P(),
            P(),
            P(None, "tensor"),
            P(None, "tensor"),
            P(None, "dp", "tensor"),
            P(None, "dp", "tensor"),
            P("tensor", "dp"),
            P("tensor", "dp"),
            P(None, "dp", "tensor"),
            P(None, "dp", "tensor"),
            P("tensor", "dp"),
            P("tensor", "dp"),
        ),
        out_specs=(
            P("dp", None),
            P("dp", None),
            P(),
            P(),
            P(),
            P(),
            P(),
            P(None, "tensor"),
            P(None, "tensor"),
            P(None, "tensor"),
            P(None, "tensor"),
            P(None, "dp", "tensor"),
            P(None, "dp", "tensor"),
            P(None, "dp", "tensor"),
            P(None, "dp", "tensor"),
            P("tensor", "dp"),
            P("tensor", "dp"),
            P("tensor", "dp"),
            P("tensor", "dp"),
            P(None, "dp", "tensor"),
            P(None, "dp", "tensor"),
            P(None, "dp", "tensor"),
            P(None, "dp", "tensor"),
            P("tensor", "dp"),
            P("tensor", "dp"),
            P("tensor", "dp"),
            P("tensor", "dp"),
        ),
        check_vma=False,
    )
```

profile of v0, /device:TPU:0, one launch (start us, length us, event | category | flops | bytes accessed | tf_op | source)
XLA Modules:
  0.0 1472.9 jit_solution(3615150835446457697)
XLA Ops:
  36.8 224.8 %all-reduce.8.cloned.1.call-done = f32[1024,1536]{1,0:T(8,128)} async-done(((f32[1024,1536]{1,0:T(8,128)}), f32[1024,1536]{1,0:T(8,128)}) %all-reduce.8.cloned.1.call-update) | async-done | bytes 6291472 | tf_op jit(solution)/shard_map/psum | solution.py:123
  268.9 17.3 %convolution_bitcast_fusion.1 = f32[2,1024,1728]{1,2,0:T(8,128)} fusion(bf16[2,1536,1728]{1,2,0:T(8,128)(2,1)} %param.28, f32[1024,1536]{1,0:T(8,128)S(1)} %get-tuple-element.146, f32[1536]{0:T(1024)S(1)} %get-tuple-element.115, f32[1024]{0:T(1024)S(1)} %add_rsqrt_fusion), kind=kOutput, calls=%fused_computation.16 | convolution fusion | flops 10876354560 | bytes 31074304 | tf_op jit(solution)/shard_map/td,sdf->stf/dot_general | solution.py:128
  286.2 16.0 %fusion.15 = (bf16[1,1024,1728]{1,2,0:T(8,128)(2,1)}, bf16[1,1024,1728]{1,2,0:T(8,128)(2,1)}, bf16[1024,1728]{0,1:T(8,128)(2,1)}) fusion(f32[2,1024,1728]{1,2,0:T(8,128)} %convolution_bitcast_fusion.1, bf16[1024,1536]{1,0:T(8,128)(2,1)S(1)} %copy-done.13, bf16[1728,1536]{1,0:T(8,128)(2,1)} %param.29), kind=kOutput, calls=%fused_computation.38 | convolution fusion | flops 5462360064 | bytes 33226752 | tf_op jit(solution)/shard_map/dot_general | solution.py:53
  302.2 16.0 %fusion.13 = f32[1024,1536]{1,0:T(8,128)} fusion(bf16[2,1536,1728]{1,2,0:T(8,128)(2,1)S(1)} %bitcast.95, bf16[1,1024,1728]{1,2,0:T(8,128)(2,1)} %get-tuple-element.150, bf16[1,1024,1728]{1,2,0:T(8,128)(2,1)} %get-tuple-element.149), kind=kOutput, calls=%fused_computation.33 | convolution fusion | flops 10875174912 | bytes 23986176 | tf_op jit(solution)/shard_map/stf,sdf->td/dot_general | solution.py:146
  318.3 10.2 convolution_convert_fusion
  328.5 211.6 %all-reduce.12.cloned.1.call-done = f32[1024,1536]{1,0:T(8,128)} async-done(((f32[1024,1536]{1,0:T(8,128)}), f32[1024,1536]{1,0:T(8,128)}) %all-reduce.12.cloned.1.call-update) | async-done | bytes 6291472 | tf_op jit(solution)/shard_map/psum | solution.py:149
  546.8 116.2 %all-reduce.10.cloned.1.call-done = bf16[1024,1536]{1,0:T(8,128)(2,1)} async-done(((bf16[1024,1536]{1,0:T(8,128)(2,1)}), bf16[1024,1536]{1,0:T(8,128)(2,1)}) %all-reduce.10.cloned.1.call-update) | async-done | bytes 3145744 | tf_op jit(solution)/shard_map/psum | solution.py:135
  663.0 9.4 multiply_add_fusion
  678.6 19.5 %convolution_bitcast_fusion = f32[2,1536,1728]{1,2,0:T(8,128)} fusion(bf16[1,1024,1728]{1,2,0:T(8,128)(2,1)} %get-tuple-element.150, bf16[1,1024,1728]{1,2,0:T(8,128)(2,1)} %get-tuple-element.149, f32[1024,1536]{1,0:T(8,128)} %copy-done.2, f32[1536]{0:T(1024)S(1)} %get-tuple-element.115, f32[1024]{0:T(1024)S(1)} %add_rsqrt_fusion), kind=kOutput, calls=%fused_computation | convolution fusion | flops 10879893504 | bytes 34613248 | tf_op jit(solution)/shard_map/td,stf->sdf/dot_general | solution.py:143
  698.1 32.6 %copy.83 = f32[2,1536,1728]{2,0,1:T(2,128)} copy(f32[2,1536,1728]{1,2,0:T(8,128)} %convolution_bitcast_fusion) | data formatting | bytes 42467328 | tf_op jit(solution)/shard_map/td,stf->sdf/transpose | solution.py:143
  747.3 6.3 convolution_bitcast_fusion.3
  753.6 11.2 fusion.55
  765.5 10.0 convolution_bitcast_fusion.2
  775.4 10.9 copy.97
  786.3 7.3 copy.104
  823.4 179.7 %all-reduce.16.cloned.1.call-done = f32[2,1536,1728]{2,0,1:T(2,128)} async-done(((f32[2,1536,1728]{2,0,1:T(2,128)}), f32[2,1536,1728]{2,0,1:T(2,128)}) %all-reduce.16.cloned.1.call-update) | async-done | bytes 21233680
  1003.1 6.7 multiply_reduce_fusion.3
  1009.7 218.6 %all-reduce.14.cloned.1.call-done = f32[1024,1536]{1,0:T(8,128)} async-done(((f32[1024,1536]{1,0:T(8,128)}), f32[1024,1536]{1,0:T(8,128)}) %all-reduce.14.cloned.1.call-update) | async-done | bytes 6291472 | tf_op jit(solution)/shard_map/psum | solution.py:186
  1233.6 25.3 %all-reduce.1 = (f32[3,384]{1,0:T(4,128)}, f32[2,1536]{1,0:T(2,128)}) all-reduce(f32[3,384]{1,0:T(4,128)} %pad_maximum_fusion.9, f32[2,1536]{1,0:T(2,128)} %pad_maximum_fusion.8), channel_id=1, replica_groups=mesh['dp'=8,'tensor'=4] {'dp'}, use_global_device_ids=true, to_apply=%region_19.0 | all-reduce | flops 4224 | bytes 33792 | tf_op jit(solution)/shard_map/psum | solution.py:190
  1262.9 9.6 fusion.9
  1272.5 43.3 %reduce-scatter.8.cloned.1.call-done = f32[1728,192]{0,1:T(8,128)} async-done(((f32[1728,1536]{0,1:T(8,128)}), f32[1728,192]{0,1:T(8,128)}) %reduce-scatter.8.cloned.1.call-update) | async-done | bytes 1327120 | tf_op jit(solution)/shard_map/reduce_scatter | solution.py:195
  1318.1 66.8 %reduce-scatter.10.cloned.1.call-done = f32[192,1152]{1,0:T(8,128)} async-done(((f32[1536,1152]{1,0:T(8,128)}), f32[192,1152]{1,0:T(8,128)}) %reduce-scatter.10.cloned.1.call-update) | async-done | bytes 884752
  1396.6 39.2 %psum.55 = f32[]{:T(128)} all-reduce(f32[]{:T(128)S(6)} %add.202), channel_id=1, replica_groups=mesh['dp'=8,'tensor'=4] {'dp','tensor'}, use_global_device_ids=true, to_apply=%region_25.0 | all-reduce | flops 1 | bytes 8 | tf_op jit(solution)/shard_map/psum | solution.py:205
  1451.6 8.9 add_multiply_fusion
  (172 shorter events, 134.2 us)
Async XLA Ops:
  7.2 254.4 %all-reduce.8.cloned.1.call-start = ((), (), s32[]{:S(2)}) async-start(), calls=%async_computation.3 | async-start | bytes 12582912 | tf_op jit(solution)/shard_map/psum | solution.py:123
  19.4 6.6 collective-permute-start
  36.6 503.5 %all-reduce.12.cloned.1.call-start = ((), (), s32[]{:S(2)}) async-start(), calls=%async_computation.5 | async-start | bytes 12582912 | tf_op jit(solution)/shard_map/psum | solution.py:149
  268.9 17.3 %copy-start.13 = (bf16[1024,1536]{1,0:T(8,128)(2,1)S(1)}, bf16[1024,1536]{1,0:T(8,128)(2,1)}, u32[]{:S(2)}) copy-start(bf16[1024,1536]{1,0:T(8,128)(2,1)} %param.23) | copy-start | bytes 9437188
  268.9 33.3 %slice-start = ((s8[10616832]{0:T(1024)(128)(4,1)}), s8[2228224]{0:T(1024)(128)(4,1)S(1)}, s32[]{:S(2)}) async-start(s8[10616832]{0:T(1024)(128)(4,1)} %bitcast.94), calls=%async_computation.11 | async-start | bytes 4456448
  268.9 33.3 %slice-start.1 = ((s8[10616832]{0:T(1024)(128)(4,1)}), s8[4194304]{0:T(1024)(128)(4,1)S(1)}, s32[]{:S(2)}) async-start(s8[10616832]{0:T(1024)(128)(4,1)} %bitcast.94), calls=%async_computation.12 | async-start | bytes 8388608
  286.2 16.0 %slice-start.2 = ((s8[10616832]{0:T(1024)(128)(4,1)}), s8[4194304]{0:T(1024)(128)(4,1)S(1)}, s32[]{:S(2)}) async-start(s8[10616832]{0:T(1024)(128)(4,1)} %bitcast.94), calls=%async_computation.13 | async-start | bytes 8388608
  318.2 344.8 %all-reduce.10.cloned.1.call-start = ((), (), s32[]{:S(2)}) async-start(), calls=%async_computation.4 | async-start | bytes 6291456 | tf_op jit(solution)/shard_map/psum | solution.py:135
  328.5 493.3 %reduce-scatter.6.cloned.1.call-start = ((), (), s32[]{:S(2)}) async-start(), calls=%async_computation.7 | async-start | bytes 2654208 | tf_op jit(solution)/shard_map/reduce_scatter | solution.py:193
  663.0 12.1 copy-start.8
  678.4 324.7 %all-reduce.16.cloned.1.call-start = ((), (), s32[]{:S(2)}) async-start(), calls=%async_computation.10 | async-start | bytes 44040192
  730.8 497.5 %all-reduce.14.cloned.1.call-start = ((), (), s32[]{:S(2)}) async-start(), calls=%async_computation.6 | async-start | bytes 12582912 | tf_op jit(solution)/shard_map/psum | solution.py:186
  737.9 3.1 collective-permute-start.1
  753.5 562.3 %reduce-scatter.8.cloned.1.call-start = ((), (), s32[]{:S(2)}) async-start(), calls=%async_computation.8 | async-start | bytes 12386304 | tf_op jit(solution)/shard_map/reduce_scatter | solution.py:195
  764.8 620.1 %reduce-scatter.10.cloned.1.call-start = ((), (), s32[]{:S(2)}) async-start(), calls=%async_computation.9 | async-start | bytes 7962624
  809.0 12.1 copy-start.40
  1441.2 9.0 copy-start.39
  1451.6 9.0 copy-start.21
  1451.6 9.0 copy-start.22
  1451.6 9.0 copy-start.23
  1451.6 10.1 copy-start.11
  1451.6 10.1 copy-start.14
  1451.6 10.1 copy-start.15
  1451.6 10.0 copy-start.16
  (30 other events, 131.0 us)
Sparse Core Ops, SparseCore 0:
  36.7 224.8 all-reduce.7
  318.3 221.7 all-reduce.11
  543.1 119.9 all-reduce.9
  678.5 41.3 reduce-scatter.5
  730.9 272.1 all-reduce.15
  1005.3 222.9 all-reduce.13
  1232.4 83.3 reduce-scatter.7
  1319.3 65.4 reduce-scatter.9
where the time goes:
time: 1480 us; the launch traced here: 1470 us
  waiting for transfers between devices  1060 us (72%)
  matrix products  123 us (8%)
  local copies, waits for them, and re-layouts  106 us (7%)
  other arithmetic  89.6 us (6%)
  blocking collectives  64.6 us (4%)
  between operations  21.5 us (1%)
    unnamed x10, waiting for transfers between devices  247 us
    psum x1, waiting for transfers between devices, body(): branch = lax.psum(branch_part, 'tensor')  225 us
    psum x1, waiting for transfers between devices, body(): grad_normed_one = lax.psum(normed_one_part, 'tensor')  219 us
    psum x1, waiting for transfers between devices, body(): grad_normed_two = lax.psum(normed_two_part, 'tensor')  212 us
    psum x1, waiting for transfers between devices, body(): lax.psum(feed_part.astype(jnp.bfloat16), 'tensor').astype(jnp.float32)  116 us
    unnamed x103, local copies, waits for them, and re-layouts  58.6 us
    reduce_scatter x1, waiting for transfers between devices, body(): lax.psum_scatter(down_part, 'dp', scatter_dimension=1, tiled=True)  43.3 us
    psum x1, blocking collectives, body(): square_total = lax.psum(local_square, ('dp', 'tensor'))  39.2 us
  transfers between devices with their start and end apart: 10, of which 8 were waited for; matrix products, arithmetic and copies ran while one was open for 13% of the time, Pallas kernels for 0%

commit v1 on v0

--- a/solution.py
+++ b/solution.py
@@ -1,6 +1,9 @@
+import functools
 import jax
 import jax.numpy as jnp
 from jax import lax
+from jax.experimental import pallas as pl
+from jax.experimental.pallas import tpu as pltpu
 from jax.sharding import PartitionSpec as P
 
 EPS_NORM = 1e-05
@@ -38,11 +41,6 @@
     return (first_next, second_next, change)
 
 
-def own_share(weight, share):
-    offset_row = lax.axis_index("dp") * share
-    return lax.dynamic_slice_in_dim(weight, offset_row, share, 1).astype(jnp.float32)
-
-
 def contract_rows(left, right):
     return lax.dot_general(
         left, right, (((0,), (0,)), ((), ())), preferred_element_type=jnp.float32
@@ -55,8 +53,511 @@
     )
 
 
-def squares(values):
-    return jnp.sum(values * values)
+ROWS_STEP = 16
+MESH = pl.DeviceIdType.MESH
+
+
+def chain_kernel(axis, depth, finish, extra_in, extra_out, *refs):
+    part_ref = refs[0]
+    ins = refs[1 : 1 + extra_in]
+    out_ref = refs[1 + extra_in]
+    outs = refs[2 + extra_in : 2 + extra_in + extra_out]
+    from_left, from_right, total, sums_send, sums_recv, back_send, back_recv = refs[
+        2 + extra_in + extra_out :
+    ]
+    count = lax.axis_size(axis)
+    me = lax.axis_index(axis)
+    last = count - 1
+    block = part_ref.shape[0] // count
+    steps = block // depth
+    ahead = min(1, steps)
+    has_left = me > 0
+    has_right = me < last
+
+    def rows(which, step):
+        return pl.ds(pl.multiple_of(which * block + step * depth, depth), depth)
+
+    def inner(step):
+        return pl.ds(pl.multiple_of(step * depth, depth), depth)
+
+    def sum_copy(right, which, step, from_part):
+        held = from_left if right else from_right
+        source = part_ref.at[rows(which, step)] if from_part else held.at[which, inner(step)]
+        lane = 0 if right else 1
+        return pltpu.make_async_remote_copy(
+            src_ref=source,
+            dst_ref=held.at[which, inner(step)],
+            send_sem=sums_send.at[lane, which, step],
+            recv_sem=sums_recv.at[lane, which, step],
+            device_id={axis: me + 1 if right else me - 1},
+            device_id_type=MESH,
+        )
+
+    def back_copy(right, which, step):
+        lane = 0 if right else 1
+        place = out_ref.at[rows(which, step)]
+        return pltpu.make_async_remote_copy(
+            src_ref=place,
+            dst_ref=place,
+            send_sem=back_send.at[lane, which, step],
+            recv_sem=back_recv.at[lane, which, step],
+            device_id={axis: me + 1 if right else me - 1},
+            device_id_type=MESH,
+        )
+
+    barrier = pltpu.get_barrier_semaphore()
+
+    @pl.when(has_left)
+    def _():
+        pl.semaphore_signal(barrier, inc=1, device_id={axis: me - 1}, device_id_type=MESH)
+
+    @pl.when(has_right)
+    def _():
+        pl.semaphore_signal(barrier, inc=1, device_id={axis: me + 1}, device_id_type=MESH)
+
+    pl.semaphore_wait(barrier, jnp.where(has_left & has_right, 2, 1))
+
+    def end_sends(step):
+        for nth in range(last):
+            @pl.when(me == 0)
+            def _():
+                sum_copy(True, last - nth, step, True).start()
+
+            @pl.when(me == last)
+            def _():
+                sum_copy(False, nth, step, True).start()
+
+    def pass_on(right, which, step):
+        held = from_left if right else from_right
+        sum_copy(right, which, step, False).wait_recv()
+        place = (which, inner(step))
+        added = held[place].astype(jnp.float32) + part_ref[rows(which, step)].astype(jnp.float32)
+        held[place] = added.astype(held.dtype)
+        sum_copy(right, which, step, False).start()
+
+    def far_end(which):
+        return jnp.maximum(which, last - which)
+
+    def when_due(step, lag, allowed, action):
+        due = step - lag
+
+        @pl.when(allowed & (due >= 0) & (due < steps))
+        def _():
+            action(due)
+
+    def total_up(step):
+        total[...] = part_ref[rows(me, step)].astype(jnp.float32)
+
+        @pl.when(has_left)
+        def _():
+            sum_copy(True, me, step, False).wait_recv()
+            total[...] += from_left[me, inner(step)].astype(jnp.float32)
+
+        @pl.when(has_right)
+        def _():
+            sum_copy(False, me, step, False).wait_recv()
+            total[...] += from_right[me, inner(step)].astype(jnp.float32)
+
+        out_ref[rows(me, step)] = finish(
+            total[...], step, rows(me, step), inner(step), ins, outs
+        ).astype(out_ref.dtype)
+
+        @pl.when(has_right)
+        def _():
+            back_copy(True, me, step).start()
+
+        @pl.when(has_left)
+        def _():
+            back_copy(False, me, step).start()
+
+    def hand_on(right, which, step):
+        back_copy(right, which, step).wait_recv()
+
+        @pl.when(has_right if right else has_left)
+        def _():
+            back_copy(right, which, step).start()
+
+    def one_step(step, carry):
+        when_due(step, -ahead, step >= 0, end_sends)
+        for nth in range(last):
+            right_to, left_to = last - nth, nth
+            when_due(
+                step, me, has_left & (me < right_to), functools.partial(pass_on, True, right_to)
+            )
+            when_due(
+                step, last - me, has_right & (me > left_to), functools.partial(pass_on, False, left_to)
+            )
+        when_due(step, far_end(me), step >= 0, total_up)
+        for far in range(1, count):
+            when_due(
+                step,
+                far_end(me - far) + far,
+                me >= far,
+                functools.partial(hand_on, True, me - far),
+            )
+            when_due(
+                step,
+                far_end(me + far) + far,
+                me + far <= last,
+                functools.partial(hand_on, False, me + far),
+            )
+        return carry
+
+    for step in range(ahead):
+        end_sends(step)
+    lax.fori_loop(0, steps + 2 * last, one_step, 0)
+
+    def sent(step, carry):
+        for which in range(count):
+            @pl.when(has_right & (me < which))
+            def _():
+                sum_copy(True, which, step, False).wait_send()
+
+            @pl.when(has_left & (me > which))
+            def _():
+                sum_copy(False, which, step, False).wait_send()
+
+            @pl.when(has_right & (me >= which))
+            def _():
+                back_copy(True, which, step).wait_send()
+
+            @pl.when(has_left & (me <= which))
+            def _():
+                back_copy(False, which, step).wait_send()
+
+        return carry
+
+    lax.fori_loop(0, steps, sent, 0)
+
+
+def chain_sum(part, ins, finish, extra_outs, number, axis="tensor"):
+    count = lax.axis_size(axis)
+    tokens, width = part.shape
+    block = tokens // count
+    depth = min(ROWS_STEP, block)
+    steps = block // depth
+    vmem = pl.BlockSpec(memory_space=pltpu.VMEM)
+    return pl.pallas_call(
+        functools.partial(chain_kernel, axis, depth, finish, len(ins), len(extra_outs)),
+        out_shape=[jax.ShapeDtypeStruct((tokens, width), jnp.bfloat16)] + list(extra_outs),
+        in_specs=[vmem] * (1 + len(ins)),
+        out_specs=[vmem] * (1 + len(extra_outs)),
+        scratch_shapes=[
+            pltpu.VMEM((count, block, width), jnp.bfloat16),
+            pltpu.VMEM((count, block, width), jnp.bfloat16),
+            pltpu.VMEM((depth, width), jnp.float32),
+            pltpu.SemaphoreType.DMA((2, count, steps)),
+            pltpu.SemaphoreType.DMA((2, count, steps)),
+            pltpu.SemaphoreType.DMA((2, count, steps)),
+            pltpu.SemaphoreType.DMA((2, count, steps)),
+        ],
+        compiler_params=pltpu.CompilerParams(collective_id=number, has_side_effects=True),
+        name="chain_sum_%d" % number,
+    )(part, *ins)
+
+
+def finish_middle(total, step, whole, own, ins, outs):
+    tokens_ref, gain_ref = ins
+    (middle_ref,) = outs
+    middle = tokens_ref[whole].astype(jnp.float32) + total
+    middle_ref[own] = middle
+    return middle * rms_scale(middle) * gain_ref[...]
+
+
+def finish_feed(total, step, whole, own, ins, outs):
+    (middle_ref,) = ins
+    return middle_ref[own] + total
+
+
+def add_gain(gain_ref, step, addend):
+    summed = jnp.sum(addend, axis=0, keepdims=True)
+
+    @pl.when(step == 0)
+    def _():
+        gain_ref[...] = summed
+
+    @pl.when(step > 0)
+    def _():
+        gain_ref[...] += summed
+
+
+def finish_middle_back(total, step, whole, own, ins, outs):
+    middle_ref, upstream_ref, gain_ref = ins
+    back_ref, gain_grad_ref = outs
+    middle = middle_ref[own]
+    inverse = rms_scale(middle)
+    normal = middle * inverse
+    add_gain(gain_grad_ref, step, total * normal)
+    back = upstream_ref[whole].astype(jnp.float32) + norm_back(
+        total, normal, inverse, gain_ref[...]
+    )
+    back_ref[own] = back
+    return back
+
+
+def finish_input_back(total, step, whole, own, ins, outs):
+    tokens_ref, middle_back_ref, gain_ref = ins
+    (gain_grad_ref,) = outs
+    tokens = tokens_ref[whole].astype(jnp.float32)
+    inverse = rms_scale(tokens)
+    normal = tokens * inverse
+    add_gain(gain_grad_ref, step, total * normal)
+    return middle_back_ref[own] + norm_back(total, normal, inverse, gain_ref[...])
+
+
+def over_dp(grad):
+    return lax.psum_scatter(grad.astype(jnp.bfloat16), "dp", scatter_dimension=0, tiled=True)
+
+
+def own_columns(weight, share):
+    return lax.dynamic_slice_in_dim(weight, lax.axis_index("dp") * share, share, 1)
+
+
+LANES = 128
+
+
+def tail_kernel(*refs):
+    gain_refs, taps_ref, share_refs = refs[0:2], refs[2], refs[3:8]
+    gains_ref, taps_sum_ref, stats_ref = refs[8:11]
+    mine, slots, joint, joint_slots, send_dp, recv_dp, send_tensor, recv_tensor = refs[11:]
+    many = lax.axis_size("dp")
+    few = lax.axis_size("tensor")
+    place = lax.axis_index("dp")
+    level = lax.axis_index("tensor")
+    width = gains_ref.shape[1]
+    spans = width // LANES
+    tap_count, tap_width = taps_ref.shape
+    tap_spans = tap_width // LANES
+    tap_start = 2 * spans
+    square_row = tap_start + tap_count * tap_spans
+
+    def peer_dp(away):
+        return lax.rem(place + away, many)
+
+    def peer_tensor(away):
+        return lax.rem(level + away, few)
+
+    def copy_dp(away, slot):
+        return pltpu.make_async_remote_copy(
+            src_ref=mine,
+            dst_ref=slots.at[slot],
+            send_sem=send_dp.at[away],
+            recv_sem=recv_dp.at[slot],
+            device_id={"dp": peer_dp(away)},
+            device_id_type=MESH,
+        )
+
+    def copy_tensor(away, slot):
+        return pltpu.make_async_remote_copy(
+            src_ref=joint,
+            dst_ref=joint_slots.at[slot],
+            send_sem=send_tensor.at[away],
+            recv_sem=recv_tensor.at[slot],
+            device_id={"tensor": peer_tensor(away)},
+            device_id_type=MESH,
+        )
+
+    barrier = pltpu.get_barrier_semaphore()
+
+    def greet_dp(away, carry):
+        pl.semaphore_signal(barrier, inc=1, device_id={"dp": peer_dp(away)}, device_id_type=MESH)
+        return carry
+
+    def greet_tensor(away, carry):
+        pl.semaphore_signal(
+            barrier, inc=1, device_id={"tensor": peer_tensor(away)}, device_id_type=MESH
+        )
+        return carry
+
+    lax.fori_loop(1, many, greet_dp, 0)
+    lax.fori_loop(1, few, greet_tensor, 0)
+    mine[...] = jnp.zeros_like(mine)
+    for which in range(2):
+        for span in range(spans):
+            mine[pl.ds(which * spans + span, 1)] = gain_refs[which][:, span * LANES : (span + 1) * LANES]
+    for tap in range(tap_count):
+        for span in range(tap_spans):
+            mine[pl.ds(tap_start + tap * tap_spans + span, 1)] = taps_ref[
+                tap : tap + 1, span * LANES : (span + 1) * LANES
+            ]
+    square = jnp.zeros((1, 1), jnp.float32)
+    for share_ref in share_refs:
+        share = share_ref[...].astype(jnp.float32)
+        square = square + jnp.sum(
+            jnp.sum(share * share, axis=0, keepdims=True), axis=1, keepdims=True
+        )
+    first = lax.broadcasted_iota(jnp.int32, (1, LANES), 1) == 0
+    mine[pl.ds(square_row, 1)] = jnp.where(first, square, 0.0)
+    pl.semaphore_wait(barrier, many + few - 2)
+
+    def start_dp(away, carry):
+        copy_dp(away, place).start()
+        return carry
+
+    def await_dp(away, carry):
+        copy_dp(away, lax.rem(place + many - away, many)).wait_recv()
+        return carry
+
+    lax.fori_loop(1, many, start_dp, 0)
+    slots[place] = mine[...]
+    lax.fori_loop(1, many, await_dp, 0)
+    joint[...] = lax.fori_loop(
+        1, many, lambda slot, summed: summed + slots[slot], slots[0]
+    )
+    taps = joint[pl.ds(tap_start, tap_count * tap_spans)]
+    tap_square = jnp.sum(jnp.sum(taps * taps, axis=0, keepdims=True), axis=1, keepdims=True)
+    joint[pl.ds(square_row, 1)] += jnp.where(first, tap_square, 0.0)
+    for tap in range(tap_count):
+        for span in range(tap_spans):
+            taps_sum_ref[tap : tap + 1, span * LANES : (span + 1) * LANES] = joint[
+                pl.ds(tap_start + tap * tap_spans + span, 1)
+            ]
+    for away in range(1, few):
+        copy_tensor(away, level).start()
+    joint_slots[level] = joint[...]
+    for away in range(1, few):
+        copy_tensor(away, lax.rem(level + few - away, few)).wait_recv()
+    summed = joint_slots[0]
+    for slot in range(1, few):
+        summed = summed + joint_slots[slot]
+    mine_gains = summed[:tap_start]
+    gain_square = jnp.sum(
+        jnp.sum(mine_gains * mine_gains, axis=0, keepdims=True), axis=1, keepdims=True
+    )
+    row = summed[square_row : square_row + 1]
+    norm = jnp.sqrt(jnp.sum(row, axis=1, keepdims=True) + gain_square)
+    stats_ref[0:1] = jnp.broadcast_to(norm, (1, LANES))
+    stats_ref[1:2] = jnp.broadcast_to(
+        jnp.minimum(1.0, CLIP_NORM / (norm + 1e-06)), (1, LANES)
+    )
+    for which in range(2):
+        for span in range(spans):
+            start = which * spans + span
+            gains_ref[which : which + 1, span * LANES : (span + 1) * LANES] = summed[
+                start : start + 1
+            ]
+
+    def sent_dp(away, carry):
+        copy_dp(away, place).wait_send()
+        return carry
+
+    lax.fori_loop(1, many, sent_dp, 0)
+    for away in range(1, few):
+        copy_tensor(away, level).wait_send()
+
+
+def tail_sums(gain_parts, taps_part, shares, number):
+    many, few = lax.axis_size("dp"), lax.axis_size("tensor")
+    width = gain_parts[0].shape[1]
+    rows = (2 * width + taps_part.size) // LANES + 1
+    rows = -(-rows // 8) * 8
+    vmem = pl.BlockSpec(memory_space=pltpu.VMEM)
+    return pl.pallas_call(
+        tail_kernel,
+        out_shape=[
+            jax.ShapeDtypeStruct((2, width), jnp.float32),
+            jax.ShapeDtypeStruct(taps_part.shape, jnp.float32),
+            jax.ShapeDtypeStruct((2, LANES), jnp.float32),
+        ],
+        in_specs=[vmem] * (3 + len(shares)),
+        out_specs=[vmem] * 3,
+        scratch_shapes=[
+            pltpu.VMEM((rows, LANES), jnp.float32),
+            pltpu.VMEM((many, rows, LANES), jnp.float32),
+            pltpu.VMEM((rows, LANES), jnp.float32),
+            pltpu.VMEM((few, rows, LANES), jnp.float32),
+            pltpu.SemaphoreType.DMA((many,)),
+            pltpu.SemaphoreType.DMA((many,)),
+            pltpu.SemaphoreType.DMA((few,)),
+            pltpu.SemaphoreType.DMA((few,)),
+        ],
+        compiler_params=pltpu.CompilerParams(collective_id=number, has_side_effects=True),
+        name="tail_sums",
+    )(*gain_parts, taps_part, *shares)
+
+
+def adam_kernel(decay, counts, place_ref, stats_ref, *refs):
+    grads, (weight_ref, first_ref, second_ref) = refs[:counts], refs[counts : counts + 3]
+    grad_ref, first_next_ref, second_next_ref, step_ref = refs[counts + 3 :]
+    factor = stats_ref[1:2, 0:1]
+
+    def update(source):
+        shape = grad_ref.shape
+        grad = source[...].astype(jnp.float32).reshape(shape)
+        master = weight_ref[...].astype(jnp.float32).reshape(shape)
+        first_next, second_next, change = adam_step(
+            master, grad, first_ref[...], second_ref[...], factor, decay
+        )
+        grad_ref[...] = grad
+        first_next_ref[...] = first_next
+        second_next_ref[...] = second_next
+        step_ref[...] = change
+
+    if counts == 1:
+        update(grads[0])
+    else:
+        for which in range(counts):
+            @pl.when(pl.program_id(0) == which)
+            def _():
+                update(grads[which])
+
+
+def adam_call(grid, grads, grad_specs, weight, weight_spec, first, second, spec, stats, place, decay):
+    return pl.pallas_call(
+        functools.partial(adam_kernel, decay, len(grads)),
+        grid_spec=pltpu.PrefetchScalarGridSpec(
+            num_scalar_prefetch=1,
+            grid=grid,
+            in_specs=[pl.BlockSpec(stats.shape, lambda *_: (0, 0))]
+            + grad_specs
+            + [weight_spec, spec, spec],
+            out_specs=[spec] * 4,
+        ),
+        out_shape=[jax.ShapeDtypeStruct(first.shape, jnp.float32)] * 4,
+        name="adam",
+    )(place, stats, *grads, weight, first, second)
+
+
+def adam_stacked(grads, weight, first, second, stats, place, pieces):
+    stack, share, width = first.shape
+    depth = share // pieces
+    grad_specs = (
+        [pl.BlockSpec((depth, width), lambda which, piece, _: (piece, which))]
+        if len(grads) == 1
+        else [
+            pl.BlockSpec(
+                (depth, width),
+                lambda which, piece, _, own=own: (
+                    jnp.where(which == own, piece, jnp.where(which < own, 0, pieces - 1)),
+                    0,
+                ),
+            )
+            for own in range(len(grads))
+        ]
+    )
+    return adam_call(
+        (stack, pieces),
+        grads,
+        grad_specs,
+        weight,
+        pl.BlockSpec(
+            (1, depth, width), lambda which, piece, place: (which, place[0] * pieces + piece, 0)
+        ),
+        first,
+        second,
+        pl.BlockSpec((1, depth, width), lambda which, piece, _: (which, piece, 0)),
+        stats,
+        place,
+        DECAY_RATE,
+    )
+
+
+def adam_flat(grad, weight, first, second, stats, place, pieces, decay):
+    rows, width = first.shape
+    spec = pl.BlockSpec((rows // pieces, width), lambda piece, _: (piece, 0))
+    return adam_call(
+        (pieces,), [grad], [spec], weight, spec, first, second, spec, stats, place, decay
+    )
 
 
 def body(
@@ -120,37 +621,41 @@
         )
     gated_rows = (streams[1] * conv_out).astype(jnp.bfloat16)
     branch_part = jnp.dot(gated_rows, mixer_weight, preferred_element_type=jnp.float32)
-    branch = lax.psum(branch_part, "tensor")
-    middle = tokens + branch
-    scale_two = rms_scale(middle)
-    normal_two = middle * scale_two
-    normed_two = (normal_two * gain_pair[1]).astype(jnp.bfloat16)
-    hidden = jnp.einsum(
-        "td,sdf->stf", normed_two, hidden_weight, preferred_element_type=jnp.float32
-    )
-    sigmoid_gate = jax.nn.sigmoid(hidden[0])
-    silu_gate = hidden[0] * sigmoid_gate
-    active = (silu_gate * hidden[1]).astype(jnp.bfloat16)
+    width = tokens_in.shape[1]
+    count = lax.axis_size("tensor")
+    own_rows = jax.ShapeDtypeStruct((tok_rows // count, width), jnp.float32)
+    gain_row = jax.ShapeDtypeStruct((1, width), jnp.float32)
+    normed_two, middle = chain_sum(
+        branch_part.astype(jnp.bfloat16), [tokens_in, gain_pair[1:2]], finish_middle, [own_rows], 1
+    )
+    gate, up = (
+        jnp.dot(normed_two, hidden_weight[which], preferred_element_type=jnp.float32)
+        for which in range(2)
+    )
+    sigmoid_gate = jax.nn.sigmoid(gate)
+    silu_gate = gate * sigmoid_gate
+    active = (silu_gate * up).astype(jnp.bfloat16)
+    grad_active = contract_cols(out_grad, down_weight)
+    grad_gate = (
+        grad_active * up * sigmoid_gate * (1.0 + gate * (1.0 - sigmoid_gate))
+    ).astype(jnp.bfloat16)
+    grad_up = (grad_active * silu_gate).astype(jnp.bfloat16)
+    normed_two_part = contract_cols(grad_gate, hidden_weight[0]) + contract_cols(
+        grad_up, hidden_weight[1]
+    )
     feed_part = jnp.dot(active, down_weight, preferred_element_type=jnp.float32)
-    feed_out = lax.psum(feed_part.astype(jnp.bfloat16), "tensor").astype(jnp.float32)
-    block_out = (middle + feed_out).astype(jnp.bfloat16)
-    upstream = out_grad.astype(jnp.float32)
-    down_part = contract_rows(active, out_grad)
-    grad_active = contract_cols(out_grad, down_weight)
-    grad_gate = grad_active * hidden[1] * sigmoid_gate * (1.0 + hidden[0] * (1.0 - sigmoid_gate))
-    grad_up = grad_active * silu_gate
-    grad_hidden = jnp.stack([grad_gate, grad_up]).astype(jnp.bfloat16)
-    hidden_part = jnp.einsum(
-        "td,stf->sdf", normed_two, grad_hidden, preferred_element_type=jnp.float32
-    )
-    normed_two_part = jnp.einsum(
-        "stf,sdf->td", grad_hidden, hidden_weight, preferred_element_type=jnp.float32
-    )
-    grad_normed_two = lax.psum(normed_two_part, "tensor")
-    gain_two_part = jnp.sum(grad_normed_two * normal_two, axis=0)
-    grad_middle = upstream + norm_back(grad_normed_two, normal_two, scale_two, gain_pair[1])
-    grad_branch = grad_middle.astype(jnp.bfloat16)
-    mixer_part = contract_rows(gated_rows, grad_branch)
+    down_share = over_dp(contract_rows(out_grad, active))
+    gate_share = over_dp(contract_rows(normed_two, grad_gate))
+    up_share = over_dp(contract_rows(normed_two, grad_up))
+    grad_branch, grad_middle, gain_two_part = chain_sum(
+        normed_two_part.astype(jnp.bfloat16),
+        [middle, out_grad, gain_pair[1:2]],
+        finish_middle_back,
+        [own_rows, gain_row],
+        2,
+    )
+    (block_out,) = chain_sum(feed_part.astype(jnp.bfloat16), [middle], finish_feed, [], 3)
+    mixer_part = contract_rows(grad_branch, gated_rows)
     grad_gated = contract_cols(grad_branch, mixer_weight)
     grad_c = grad_gated * conv_out
     grad_conv = (grad_gated * streams[1]).astype(jnp.bfloat16)
@@ -177,96 +682,72 @@
     grad_streams = jnp.stack([grad_product * streams[2], grad_c, grad_product * streams[0]]).astype(
         jnp.bfloat16
     )
-    stream_part = jnp.einsum(
-        "td,stc->sdc", normed_one, grad_streams, preferred_element_type=jnp.float32
-    )
     normed_one_part = jnp.einsum(
         "stc,sdc->td", grad_streams, stream_weight, preferred_element_type=jnp.float32
     )
-    grad_normed_one = lax.psum(normed_one_part, "tensor")
-    gain_one_part = jnp.sum(grad_normed_one * normal_one, axis=0)
-    input_grad = grad_middle + norm_back(grad_normed_one, normal_one, scale_one, gain_pair[0])
-    gain_stack = jnp.stack([gain_one_part, gain_two_part])
-    gains_grad, taps_grad = lax.psum((gain_stack, taps_part), "dp")
-    stream_total, mixer_total, hidden_total, down_total = (
-        lax.psum_scatter(stream_part, "dp", scatter_dimension=1, tiled=True),
-        lax.psum_scatter(mixer_part, "dp", scatter_dimension=1, tiled=True),
-        lax.psum_scatter(hidden_part, "dp", scatter_dimension=1, tiled=True),
-        lax.psum_scatter(down_part, "dp", scatter_dimension=1, tiled=True),
-    )
-    first_dp = (lax.axis_index("dp") == 0).astype(jnp.float32)
-    first_tensor = (lax.axis_index("tensor") == 0).astype(jnp.float32)
-    local_square = (
-        squares(stream_total) + squares(mixer_total) + squares(hidden_total) + squares(down_total)
-    )
-    local_square = local_square + first_dp * (
-        squares(taps_grad) + first_tensor * squares(gains_grad)
-    )
-    square_total = lax.psum(local_square, ("dp", "tensor"))
-    grad_norm = jnp.sqrt(square_total)
-    factor = jnp.minimum(1.0, CLIP_NORM / (grad_norm + 1e-06))
-    gains_out = adam_step(gain_pair, gains_grad, gains_first, gains_second, factor, 0.0)
-    taps_out = adam_step(tap_values, taps_grad, taps_first, taps_second, factor, DECAY_RATE)
-    stream_out = adam_step(
-        own_share(stream_weight, stream_total.shape[1]),
-        stream_total,
-        stream_first,
-        stream_second,
-        factor,
-        DECAY_RATE,
-    )
-    mixer_out = adam_step(
-        own_share(mixer_weight, mixer_total.shape[1]),
-        mixer_total,
+    mixer_share = over_dp(mixer_part)
+    stream_cols = jnp.concatenate(
+        [contract_rows(normed_one, grad_streams[which]) for which in range(3)], 1
+    )
+    stream_share = over_dp(stream_cols)
+    input_back, gain_one_part = chain_sum(
+        normed_one_part.astype(jnp.bfloat16),
+        [tokens_in, grad_middle, gain_pair[0:1]],
+        finish_input_back,
+        [gain_row],
+        4,
+    )
+    input_grad = input_back.astype(jnp.float32)
+    gains_sum, taps_sum, stats = tail_sums(
+        [gain_one_part, gain_two_part],
+        taps_part,
+        [stream_share, mixer_share, gate_share, up_share, down_share],
+        5,
+    )
+    grad_norm = stats[0, 0]
+    place = lax.axis_index("dp").astype(jnp.int32)[None]
+    gains_out = adam_flat(
+        gains_sum, norm_gains, gains_first, gains_second, stats, place, 1, 0.0
+    )
+    taps_out = adam_flat(
+        taps_sum, conv_taps, taps_first, taps_second, stats, place, 1, DECAY_RATE
+    )
+    stream_out = adam_stacked(
+        [stream_share], stream_weight, stream_first, stream_second, stats, place, 1
+    )
+    mixer_out = adam_flat(
+        mixer_share.T,
+        own_columns(mixer_weight, mixer_first.shape[1]),
         mixer_first,
         mixer_second,
-        factor,
+        stats,
+        place,
+        1,
         DECAY_RATE,
     )
-    hidden_out = adam_step(
-        own_share(hidden_weight, hidden_total.shape[1]),
-        hidden_total,
-        hidden_first,
-        hidden_second,
-        factor,
-        DECAY_RATE,
-    )
-    down_out = adam_step(
-        own_share(down_weight, down_total.shape[1]),
-        down_total,
+    hidden_out = adam_stacked(
+        [gate_share, up_share], hidden_weight, hidden_first, hidden_second, stats, place, 3
+    )
+    down_out = adam_flat(
+        down_share.T,
+        own_columns(down_weight, down_first.shape[1]),
         down_first,
         down_second,
-        factor,
+        stats,
+        place,
+        6,
         DECAY_RATE,
     )
     return (
         block_out,
         input_grad,
         grad_norm,
-        gains_grad,
-        gains_out[0],
-        gains_out[1],
-        gains_out[2],
-        taps_grad,
-        taps_out[0],
-        taps_out[1],
-        taps_out[2],
-        stream_total,
-        stream_out[0],
-        stream_out[1],
-        stream_out[2],
-        mixer_total,
-        mixer_out[0],
-        mixer_out[1],
-        mixer_out[2],
-        hidden_total,
-        hidden_out[0],
-        hidden_out[1],
-        hidden_out[2],
-        down_total,
-        down_out[0],
-        down_out[1],
-        down_out[2],
+        *gains_out,
+        *taps_out,
+        *stream_out,
+        *mixer_out,
+        *hidden_out,
+        *down_out,
     )
 
 

time: 1480 us -> 665 us (0.45)
  waiting for transfers between devices: 1060 us -> 0.11 us
  Pallas kernels: 0 us -> 419 us
  other arithmetic: 89.6 us -> 24.2 us
  blocking collectives: 64.6 us -> 0 us
  local copies, waits for them, and re-layouts: 106 us -> 64.1 us
    psum x4 -> x0, waiting for transfers between devices: 771 us -> none  [the longest x1 225 us: body(): branch = lax.psum(branch_part, 'tensor')]
    pallas_call x0 -> x11, Pallas kernels: none -> 419 us  [the longest x4 378 us: chain_sum(): pl.pallas_call(functools.partial(chain_kernel, axis, depth, finish, len(i...]
    unnamed x10 -> x5, waiting for transfers between devices: 247 us -> 0.08 us
    psum x2 -> x0, blocking collectives: 64.6 us -> none  [the longest x1 39.2 us: body(): square_total = lax.psum(local_square, ('dp', 'tensor'))]
    reduce_scatter x2 -> x5, waiting for transfers between devices: 43.4 us -> 0.02 us  [over_dp(): lax.psum_scatter(grad.astype(jnp.bfloat16), 'dp', scatter_dimension=0, ti...]
    dot_general x4 -> x2, matrix products: 62.8 us -> 26.8 us  [body(): jnp.dot(normed_two, hidden_weight[which], preferred_element_type=jnp.floa...]
    transpose x1 -> x0, local copies, waits for them, and re-layouts: 32.6 us -> none  [body(): jnp.einsum('td,stf->sdf', normed_two, grad_hidden, preferred_element_type...]
    reduce_sum x8 -> x0, other arithmetic: 26.2 us -> none  [the longest x6 15.4 us: squares(): return jnp.sum(values * values)]
  transfers between devices with their start and end apart: 10 -> 7, of which waited for: 8 -> 0; matrix products, arithmetic and copies ran while one was open for 13% -> 18% of each run, Pallas kernels for 0% -> 29%
where the time goes in v1:
time: 665 us; the launch traced here: 657 us
  Pallas kernels  419 us (63%)
  matrix products  131 us (20%)
  local copies, waits for them, and re-layouts  64.1 us (10%)
  other arithmetic  24.2 us (4%)
  between operations  14.7 us (2%)
    pallas_call x4, Pallas kernels, chain_sum(): pl.pallas_call(functools.partial(chain_kernel, axis, depth, finish, len(i...  378 us
    unnamed x83, local copies, waits for them, and re-layouts  57.6 us
    dot_general x7, matrix products, contract_rows(): lax.dot_general(left, right, (((0,), (0,)), ((), ())), preferred_element_...  40.4 us
    dot_general x4, matrix products, contract_cols(): lax.dot_general(left, right, (((1,), (1,)), ((), ())), preferred_element_...  35.4 us
    pallas_call x6, Pallas kernels, adam_call(): pl.pallas_call(functools.partial(adam_kernel, decay, len(grads)), grid_sp...  28 us
    dot_general x2, matrix products, body(): jnp.dot(normed_two, hidden_weight[which], preferred_element_type=jnp.floa...  26.8 us
  transfers between devices with their start and end apart: 7, of which 0 were waited for; matrix products, arithmetic and copies ran while one was open for 18% of the time, Pallas kernels for 29%

profile of v1, /device:TPU:0, one launch (start us, length us, event | category | flops | bytes accessed | tf_op | source)
XLA Modules:
  0.0 657.3 jit_solution(12985818579309094301)
XLA Ops:
  10.9 6.3 fusion.26
  23.9 10.7 %fusion.44 = f32[1024,1728]{0,1:T(8,128)} fusion(bf16[1024,1536]{1,0:T(8,128)(2,1)} %refs_2_.7, bf16[1728,1536]{1,0:T(8,128)(2,1)} %param.29), kind=kOutput, calls=%fused_computation.82 | convolution fusion | flops 5435817984 | bytes 15532032 | tf_op jit(solution)/shard_map/dot_general | solution.py:51
  42.9 96.5 %chain_sum_1.1 = (bf16[1024,1536]{1,0:T(8,128)(2,1)}, f32[256,1536]{1,0:T(8,128)}) custom-call(bf16[1024,1536]{1,0:T(8,128)(2,1)} %convolution_convert_fusion.4.refs_0_, bf16[1024,1536]{1,0:T(8,128)(2,1)} %refs_1_.6, f32[1,1536]{1,0:T(1,128)} %get-tuple-element.171.refs_2_.refs_3_), custom_call_target="tpu_custom_call" | custom-call | tf_op jit(solution)/shard_map/chain_sum_1/pallas_call | solution.py:240
  139.4 10.9 %fusion.7 = f32[1024,1728]{0,1:T(8,128)} fusion(bf16[1024,1536]{1,0:T(8,128)(2,1)} %get-tuple-element.61, bf16[2,1536,1728]{1,2,0:T(8,128)(2,1)} %param.28), kind=kOutput, calls=%fused_computation.18 | convolution fusion | flops 5435817984 | bytes 15532032 | tf_op jit(solution)/shard_map/dot_general | solution.py:632
  150.4 15.9 %multiply_convert_fusion.1 = (bf16[1024,1728]{0,1:T(8,128)(2,1)S(1)}, bf16[1024,1728]{0,1:T(8,128)(2,1)}, bf16[1024,1728]{0,1:T(8,128)(2,1)}) fusion(f32[1024,1728]{0,1:T(8,128)} %fusion.44, f32[1024,1728]{0,1:T(8,128)} %fusion.7, bf16[1024,1536]{1,0:T(8,128)(2,1)S(1)} %copy-done.30, bf16[2,1536,1728]{1,2,0:T(8,128)(2,1)} %param.28), kind=kOutput, calls=%fused_computation.6 | convolution fusion | flops 5462360064 | bytes 33226752 | tf_op jit(solution)/shard_map/dot_general | solution.py:632
  166.2 10.4 %fusion.5 = f32[1024,1536]{1,0:T(8,128)S(1)} fusion(bf16[1024,1728]{0,1:T(8,128)(2,1)} %get-tuple-element.160, bf16[2,1536,1728]{1,2,0:T(8,128)(2,1)} %param.28), kind=kOutput, calls=%fused_computation.16 | convolution fusion | flops 5435817984 | bytes 15138816 | tf_op jit(solution)/shard_map/dot_general | solution.py:51
  176.7 10.4 %add_convert_fusion.refs_0_ = bf16[1024,1536]{1,0:T(8,128)(2,1)} fusion(f32[1024,1536]{1,0:T(8,128)S(1)} %fusion.5, bf16[1024,1728]{0,1:T(8,128)(2,1)S(1)} %get-tuple-element.159, bf16[2,1536,1728]{1,2,0:T(8,128)(2,1)} %param.28), kind=kOutput, calls=%fused_computation.15 | convolution fusion | flops 5438963712 | bytes 18284544 | tf_op jit(solution)/shard_map/dot_general | solution.py:51
  187.1 94.0 %chain_sum_2.1 = (bf16[1024,1536]{1,0:T(8,128)(2,1)}, f32[256,1536]{1,0:T(8,128)}, f32[1,1536]{1,0:T(1,128)}) custom-call(bf16[1024,1536]{1,0:T(8,128)(2,1)} %add_convert_fusion.refs_0_, f32[256,1536]{1,0:T(8,128)} %get-tuple-element.62.refs_1_, bf16[1024,1536]{1,0:T(8,128)(2,1)} %refs_2_.7, f32[1,1536]{1,0:T(1,128)} %get-tuple-element.171.refs_2_.refs_3_), custom_call_target="tpu_custom_call" | custom-call | tf_op jit(solution)/shard_map/chain_sum_2/pallas_call | solution.py:240
  281.1 3.8 fusion.45
  307.5 10.1 %convolution_convert_fusion.2 = bf16[1536,1728]{1,0:T(8,128)(2,1)} fusion(bf16[1024,1536]{1,0:T(8,128)(2,1)} %get-tuple-element.61, bf16[1024,1728]{0,1:T(8,128)(2,1)} %copy-done.32), kind=kOutput, calls=%fused_computation.4 | convolution fusion | flops 5438472192 | bytes 11993088 | tf_op jit(solution)/shard_map/dot_general | solution.py:45
  317.7 10.2 %convolution_convert_fusion.1 = bf16[1536,1728]{1,0:T(8,128)(2,1)} fusion(bf16[1024,1536]{1,0:T(8,128)(2,1)} %get-tuple-element.61, bf16[1024,1728]{0,1:T(8,128)(2,1)} %get-tuple-element.160), kind=kOutput, calls=%fused_computation.3 | convolution fusion | flops 5438472192 | bytes 11993088 | tf_op jit(solution)/shard_map/dot_general | solution.py:45
  328.0 10.1 %fusion.1 = bf16[1536,1728]{0,1:T(8,128)(2,1)} fusion(bf16[1024,1728]{0,1:T(8,128)(2,1)} %get-tuple-element.161, bf16[1024,1536]{1,0:T(8,128)(2,1)} %refs_2_.7), kind=kOutput, calls=%fused_computation.10 | convolution fusion | flops 5438472192 | bytes 11993088 | tf_op jit(solution)/shard_map/dot_general | solution.py:45
  338.1 8.3 %copy.91 = bf16[1536,1728]{1,0:T(8,128)(2,1)} copy(bf16[1536,1728]{0,1:T(8,128)(2,1)} %fusion.1) | data formatting | bytes 10616832
  346.5 14.4 %copy.75.refs_2_ = bf16[2,1536,1728]{2,1,0:T(8,128)(2,1)} copy(bf16[2,1536,1728]{1,2,0:T(8,128)(2,1)} %param.28) | data formatting | bytes 21233664 | tf_op args[7]
  371.0 10.2 %convolution_convert_fusion.3.refs_0_ = bf16[1024,1536]{1,0:T(8,128)(2,1)} fusion(bf16[1024,1728]{0,1:T(8,128)(2,1)} %get-tuple-element.161, bf16[1728,1536]{1,0:T(8,128)(2,1)} %param.29), kind=kOutput, calls=%fused_computation.28 | convolution fusion | flops 5437390848 | bytes 11993088 | tf_op jit(solution)/shard_map/dot_general | solution.py:646
  381.1 92.8 %chain_sum_3.1 = bf16[1024,1536]{1,0:T(8,128)(2,1)} custom-call(bf16[1024,1536]{1,0:T(8,128)(2,1)} %convolution_convert_fusion.3.refs_0_, f32[256,1536]{1,0:T(8,128)} %get-tuple-element.62.refs_1_), custom_call_target="tpu_custom_call" | custom-call | tf_op jit(solution)/shard_map/chain_sum_3/pallas_call | solution.py:240
  474.0 8.2 %bitcast_convert_fusion.refs_0_ = bf16[1024,1536]{1,0:T(8,128)(2,1)} fusion(bf16[3,1536,384]{2,1,0:T(8,128)(2,1)} %refs_1_.9, bf16[1,1024,384]{2,1,0:T(8,128)(2,1)S(1)} %bitcast.80, bf16[1,1024,384]{2,1,0:T(8,128)(2,1)S(1)} %bitcast.78, bf16[1,1024,384]{2,1,0:T(8,128)(2,1)} %bitcast.81), kind=kOutput, calls=%fused_computation.14 | convolution fusion | flops 3627810816 | bytes 9043968 | tf_op jit(solution)/shard_map/stc,sdc->td/dot_general | solution.py:685
  482.1 94.7 %chain_sum_4.1 = (bf16[1024,1536]{1,0:T(8,128)(2,1)}, f32[1,1536]{1,0:T(1,128)}) custom-call(bf16[1024,1536]{1,0:T(8,128)(2,1)} %bitcast_convert_fusion.refs_0_, bf16[1024,1536]{1,0:T(8,128)(2,1)} %refs_1_.6, f32[256,1536]{1,0:T(8,128)} %get-tuple-element.64.refs_2_, f32[1,1536]{1,0:T(1,128)} %get-tuple-element.170.refs_3_), custom_call_target="tpu_custom_call" | custom-call | tf_op jit(solution)/shard_map/chain_sum_4/pallas_call | solution.py:240
  576.8 5.5 convert_element_type.104
  584.7 13.1 %tail_sums.1 = (f32[2,1536]{1,0:T(2,128)}, f32[3,384]{1,0:T(4,128)}, f32[2,128]{1,0:T(2,128)}) custom-call(f32[1,1536]{1,0:T(1,128)} %get-tuple-element.66.refs_0_, f32[1,1536]{1,0:T(1,128)} %get-tuple-element.67.refs_1_, f32[3,384]{1,0:T(4,128)} %pad_maximum_fusion.1.refs_2_, bf16[192,1152]{1,0:T(8,128)(2,1)} %reduce-scatter.10.cloned.1.call-done.refs_3_.refs_0_, ...), custom_call_target="tpu_custom_call" | custom-call | tf_op jit(solution)/shard_map/tail_sums/pallas_call | solution.py:455
  600.2 7.3 %adam.11 = (f32[1728,192]{1,0:T(8,128)}, f32[1728,192]{1,0:T(8,128)}, f32[1728,192]{1,0:T(8,128)}, f32[1728,192]{1,0:T(8,128)}) custom-call(s32[1]{0:T(128)} %bitcast.13.place_ref, f32[2,128]{1,0:T(2,128)} %get-tuple-element.68.stats_ref, bf16[1728,192]{1,0:T(8,128)(2,1)} %bitcast.77, bf16[1728,192]{1,0:T(8,128)(2,1)} %constant_dynamic-slice_fusion.refs_1_, ...), custom_call_target="tpu_custom_call" | custom-call | tf_op jit(solution)/shard_map/adam/pallas_call | solution.py:506
  631.3 4.6 adam.8
  635.9 10.7 %adam.10 = (f32[2,192,1728]{2,1,0:T(8,128)}, f32[2,192,1728]{2,1,0:T(8,128)}, f32[2,192,1728]{2,1,0:T(8,128)}, f32[2,192,1728]{2,1,0:T(8,128)}) custom-call(s32[1]{0:T(128)} %bitcast.13.place_ref, f32[2,128]{1,0:T(2,128)} %get-tuple-element.68.stats_ref, bf16[192,1728]{1,0:T(8,128)(2,1)} %reduce-scatter.12.cloned.1.call-done.refs_5_.refs_0_, ...), custom_call_target="tpu_custom_call" | custom-call | tf_op jit(solution)/shard_map/adam/pallas_call | solution.py:506
  646.6 3.8 copy.94
  (134 shorter events, 79.8 us)
Async XLA Ops:
  7.2 32.2 %copy-start = (bf16[384,1536]{1,0:T(8,128)(2,1)S(1)}, bf16[384,1536]{1,0:T(8,128)(2,1)}, u32[]{:S(2)}) copy-start(bf16[384,1536]{1,0:T(8,128)(2,1)} %param.27) | copy-start | bytes 3538948
  7.2 575.7 %reduce-scatter.16.cloned.1.call-start = ((), (), s32[]{:S(2)}) async-start(), calls=%async_computation.8 | async-start | bytes 1327104 | tf_op jit(solution)/shard_map/reduce_scatter | solution.py:309
  8.1 9.1 %copy-start.24 = (f32[1536]{0:T(1024)}, f32[1536]{0:T(1024)S(1)}, u32[]{:S(2)}) copy-start(f32[1536]{0:T(1024)S(1)} %slice_reduce_fusion.3) | copy-start | bytes 18436
  10.9 6.3 copy-start.27
  19.4 4.4 copy-start.19
  19.6 15.7 %collective-permute-start = (bf16[2,384]{1,0:T(2,128)(2,1)S(1)}, bf16[2,384]{1,0:T(2,128)(2,1)}, u32[]{:S(2)}, u32[]{:S(2)}) collective-permute-start(bf16[2,384]{1,0:T(2,128)(2,1)S(1)} %slice.119), channel_id=1, source_target_pairs={{0,4},{4,8},{8,12},{12,16},{16,20},{20,24},{24,28},{1,5},{5,9},{9,... | collective-permute-start | bytes 4616 | tf_op jit(solution)/shard_map/ppermute | solution.py:22
  23.9 12.3 %copy-start.20 = (f32[384]{0:T(512)S(1)}, f32[384]{0:T(512)}, u32[]{:S(2)}) copy-start(f32[384]{0:T(512)} %get-tuple-element.152) | copy-start | bytes 4612
  23.9 12.3 %copy-start.21 = (f32[384]{0:T(512)S(1)}, f32[384]{0:T(512)}, u32[]{:S(2)}) copy-start(f32[384]{0:T(512)} %get-tuple-element.153) | copy-start | bytes 4612
  23.9 12.3 %copy-start.22 = (f32[384]{0:T(512)S(1)}, f32[384]{0:T(512)}, u32[]{:S(2)}) copy-start(f32[384]{0:T(512)} %get-tuple-element.154) | copy-start | bytes 4612
  35.3 4.1 copy-start.18
  139.4 10.9 %copy-start.30 = (bf16[1024,1536]{1,0:T(8,128)(2,1)S(1)}, bf16[1024,1536]{1,0:T(8,128)(2,1)}, u32[]{:S(2)}) copy-start(bf16[1024,1536]{1,0:T(8,128)(2,1)} %get-tuple-element.61) | copy-start | bytes 9437188
  166.2 10.5 %copy-start.32 = (bf16[1024,1728]{0,1:T(8,128)(2,1)}, bf16[1024,1728]{0,1:T(8,128)(2,1)S(1)}, u32[]{:S(2)}) copy-start(bf16[1024,1728]{0,1:T(8,128)(2,1)S(1)} %get-tuple-element.159) | copy-start | bytes 10616836
  287.0 5.0 copy-start.10
  287.6 7.3 %collective-permute-start.1 = (bf16[2,384]{1,0:T(2,128)(2,1)}, bf16[2,384]{1,0:T(2,128)(2,1)}, u32[]{:S(2)}, u32[]{:S(2)}) collective-permute-start(bf16[2,384]{1,0:T(2,128)(2,1)} %slice.126), channel_id=1, source_target_pairs={{4,0},{8,4},{12,8},{16,12},{20,16},{24,20},{28,24},{5,1},{9,5},{13... | collective-permute-start | bytes 4616 | tf_op jit(solution)/shard_map/ppermute | solution.py:22
  294.9 289.7 %reduce-scatter.10.cloned.1.call-start = ((), (), s32[]{:S(2)}) async-start(), calls=%async_computation.5 | async-start | bytes 3981312 | tf_op jit(solution)/shard_map/reduce_scatter | solution.py:309
  298.7 4.8 copy-start.14
  307.5 277.2 %reduce-scatter.12.cloned.1.call-start = ((), (), s32[]{:S(2)}) async-start(), calls=%async_computation.6 | async-start | bytes 6193152 | tf_op jit(solution)/shard_map/reduce_scatter | solution.py:309
  317.7 267.0 %reduce-scatter.14.cloned.1.call-start = ((), (), s32[]{:S(2)}) async-start(), calls=%async_computation.7 | async-start | bytes 6193152 | tf_op jit(solution)/shard_map/reduce_scatter | solution.py:309
  328.0 256.7 %reduce-scatter.18.cloned.1.call-start = ((), (), s32[]{:S(2)}) async-start(), calls=%async_computation.9 | async-start | bytes 6193152 | tf_op jit(solution)/shard_map/reduce_scatter | solution.py:309
  346.4 14.4 %copy-start.8 = (f32[1728,192]{0,1:T(8,128)S(1)}, f32[1728,192]{0,1:T(8,128)}, u32[]{:S(2)}) copy-start(f32[1728,192]{0,1:T(8,128)} %param.40) | copy-start | bytes 3981316
  362.6 4.1 copy-start.16
  381.1 92.8 %copy-start.11 = (bf16[1024,384]{1,0:T(8,128)(2,1)S(1)}, bf16[1024,384]{1,0:T(8,128)(2,1)}, u32[]{:S(2)}) copy-start(bf16[1024,384]{1,0:T(8,128)(2,1)} %copy-done.10) | copy-start | bytes 2359300
  584.7 14.3 %copy-start.6 = (bf16[192,1728]{1,0:T(8,128)(2,1)S(1)}, bf16[192,1728]{1,0:T(8,128)(2,1)}, u32[]{:S(2)}) copy-start(bf16[192,1728]{1,0:T(8,128)(2,1)} %reduce-scatter.18.cloned.1.call-done.refs_7_) | copy-start | bytes 1990660
  610.5 6.3 copy-start.7
  (16 other events, 51.5 us)
Sparse Core Ops, SparseCore 0:
  295.0 36.2 reduce-scatter.15
  334.8 47.9 reduce-scatter.9
  386.3 57.7 reduce-scatter.11
  447.4 57.7 reduce-scatter.13
  508.5 57.7 reduce-scatter.17
